TPU v7x, 32 devices: a whole 2x2x4 slice. The times are simulated.
32 devices in a mesh: img: 4 (over x, core), head: 2 (over y), txt: 4 (over z).
Axes of the slice: x: 2, y: 2, z: 4, core: 2. Of those that a mesh axis runs over, the one named last changes fastest.
Arguments:
- image_feats: bfloat16 [4096, 7680], P(('img', 'txt'), 'head'), may hold values from -6 to 6
- key_weight: bfloat16 [7680, 512], P('head'), may hold values from -0.0625 to 0.0625
- value_weight: bfloat16 [7680, 512], P('head'), may hold values from -0.0625 to 0.0625
- queries: bfloat16 [1024, 4096], P('txt', 'head'), may hold values from -21 to 21
- grad_out: bfloat16 [1024, 4096], P('txt', 'head'), may hold values from -768 to 768
- tile_image: int32 [32], P('img'), may hold values from 0 to 7, never falling along the last dimension, each value on 1 to 8 neighbouring positions
- text_sees: int32 [8, 8], replicated, may hold values from 0 to 1, as said below
Outputs:
- attn_out: bfloat16 [1024, 4096], P('txt', 'head')
- grad_feats: bfloat16 [4096, 7680], P(('img', 'txt'), 'head')
Inputs may be any that keep to these rules, and one draw needn't show every extreme that they name: `text_sees`: every row holds at least one 1.
All inputs are finite; a program needn't handle non-finite values.
Results may differ from a plain program's by a relative error of at most 0.012.
The roundings to bfloat16 on the way count: a program that leaves them out, or rounds other values in their place, can miss the bound.
Values may be sent and summed in bfloat16 or wider, within the bound.
A program may use at most 128 MiB of HBM per device.

v0:
```python
import math

import jax
import jax.numpy as jnp
from jax import lax
from jax.sharding import PartitionSpec as P

HD = 128
TILE = 128
TBLK = 128


def build_mask(text_sees, tile_image, text_count):
    blocks_total = text_sees.shape[0]
    images_total = text_sees.shape[1]
    text_rows = lax.axis_index("txt") * text_count + jnp.arange(text_count, dtype=jnp.int32)
    text_block = text_rows // TBLK
    block_onehot = (
        text_block[:, None] == jnp.arange(blocks_total, dtype=jnp.int32)[None, :]
    ).astype(jnp.float32)
    row_sees = jnp.dot(block_onehot, text_sees.astype(jnp.float32))
    tile_onehot = (
        tile_image[:, None] == jnp.arange(images_total, dtype=jnp.int32)[None, :]
    ).astype(jnp.float32)
    tile_allowed = jnp.dot(row_sees, tile_onehot.T) > 0.5
    return jnp.repeat(tile_allowed, TILE, axis=1)


def shards(image_feats, key_weight, value_weight, queries, grad_out, tile_image, text_sees):
    key_part = jnp.dot(image_feats, key_weight, preferred_element_type=jnp.float32)
    value_part = jnp.dot(image_feats, value_weight, preferred_element_type=jnp.float32)
    key_own, value_own = (
        lax.psum_scatter(key_part, "head", scatter_dimension=1, tiled=True),
        lax.psum_scatter(value_part, "head", scatter_dimension=1, tiled=True),
    )
    keys, values = (
        lax.all_gather(key_own.astype(jnp.bfloat16), "txt", axis=0, tiled=True),
        lax.all_gather(value_own.astype(jnp.bfloat16), "txt", axis=0, tiled=True),
    )
    text_count = queries.shape[0]
    key_count = keys.shape[0]
    groups = keys.shape[1] // HD
    repeats = queries.shape[1] // (groups * HD)
    scale_factor = 1.0 / math.sqrt(HD)
    allowed = build_mask(text_sees, tile_image, text_count)
    query_heads = queries.reshape(text_count, groups, repeats, HD)
    grad_heads = grad_out.reshape(text_count, groups, repeats, HD)
    key_heads = keys.reshape(key_count, groups, HD)
    value_heads = values.reshape(key_count, groups, HD)
    scores = (
        jnp.einsum("tgrd,jgd->grtj", query_heads, key_heads, preferred_element_type=jnp.float32)
        * scale_factor
    )
    masked = jnp.where(allowed[None, None], scores, -1e30)
    row_max = lax.pmax(jnp.max(masked, axis=-1), "img")
    weights = jnp.exp(masked - row_max[..., None]).astype(jnp.bfloat16)
    local_totals = (
        jnp.sum(weights, axis=-1, dtype=jnp.float32)
        .transpose(2, 0, 1)
        .reshape(text_count, groups * repeats)
    )
    numerator = jnp.einsum(
        "grtj,jgd->tgrd", weights, value_heads, preferred_element_type=jnp.float32
    )
    numerator = numerator.reshape(text_count, groups * repeats, HD)
    num_rows = lax.psum_scatter(numerator, "img", scatter_dimension=0, tiled=True)
    totals = lax.psum(local_totals, "img")
    share_rows = num_rows.shape[0]
    row_totals = lax.dynamic_slice_in_dim(totals, lax.axis_index("img") * share_rows, share_rows, 0)
    out_rows = (
        (num_rows / row_totals[..., None])
        .astype(jnp.bfloat16)
        .reshape(share_rows, groups * repeats * HD)
    )
    attn_out = lax.all_gather(out_rows, "img", axis=0, tiled=True)
    log_total = row_max + jnp.log(totals.reshape(text_count, groups, repeats).transpose(1, 2, 0))
    products = grad_out.astype(jnp.float32) * attn_out.astype(jnp.float32)
    row_delta = jnp.sum(products.reshape(text_count, groups, repeats, HD), axis=-1).transpose(
        1, 2, 0
    )
    key_grads = []
    value_grads = []
    for group_index in range(groups):
        probabilities = jnp.exp(masked[group_index] - log_total[group_index][..., None])
        grad_probs = jnp.einsum(
            "trd,jd->rtj",
            grad_heads[:, group_index],
            value_heads[:, group_index],
            preferred_element_type=jnp.float32,
        )
        grad_scores = (
            probabilities * (grad_probs - row_delta[group_index][..., None]) * scale_factor
        ).astype(jnp.bfloat16)
        value_grads.append(
            jnp.einsum(
                "rtj,trd->jd",
                probabilities.astype(jnp.bfloat16),
                grad_heads[:, group_index],
                preferred_element_type=jnp.float32,
            )
        )
        key_grads.append(
            jnp.einsum(
                "rtj,trd->jd",
                grad_scores,
                query_heads[:, group_index],
                preferred_element_type=jnp.float32,
            )
        )
    key_grad = jnp.concatenate(key_grads, axis=1)
    value_grad = jnp.concatenate(value_grads, axis=1)
    key_own_grad, value_own_grad = (
        lax.psum_scatter(key_grad, "txt", scatter_dimension=0, tiled=True),
        lax.psum_scatter(value_grad, "txt", scatter_dimension=0, tiled=True),
    )
    key_all, value_all = (
        lax.all_gather(key_own_grad.astype(jnp.bfloat16), "head", axis=1, tiled=True),
        lax.all_gather(value_own_grad.astype(jnp.bfloat16), "head", axis=1, tiled=True),
    )
    contract = (((1,), (1,)), ((), ()))
    grad_feats = lax.dot_general(key_all, key_weight, contract, preferred_element_type=jnp.float32)
    grad_feats = grad_feats + lax.dot_general(
        value_all, value_weight, contract, preferred_element_type=jnp.float32
    )
    return (attn_out, grad_feats.astype(jnp.bfloat16))


def solution(mesh):
    placed = (
        P(("img", "txt"), "head"),
        P("head", None),
        P("head", None),
        P("txt", "head"),
        P("txt", "head"),
        P("img"),
        P(),
    )
    return jax.shard_map(
        shards,
        mesh=mesh,
        in_specs=placed,
        out_specs=(P("txt", "head"), P(("img", "txt"), "head")),
        check_vma=False,
    )
```

profile of v0, /device:TPU:0, one launch (start us, length us, event | category | flops | bytes accessed | tf_op | source)
XLA Modules:
  0.0 229.2 jit_solution(3940299989447517550)
XLA Ops:
  7.2 1.5 copy-done
  8.7 4.1 %fusion.57 = f32[256,512]{1,0:T(8,128)} fusion(bf16[256,3840]{1,0:T(8,128)(2,1)S(1)} %copy-done, bf16[3840,512]{1,0:T(8,128)(2,1)} %param.8), kind=kOutput, calls=%fused_computation.67 | convolution fusion | flops 1006632960 | bytes 6422528 | tf_op jit(solution)/shard_map/dot_general | solution.py:30
  12.9 4.1 %fusion.56 = f32[256,512]{1,0:T(8,128)} fusion(bf16[256,3840]{1,0:T(8,128)(2,1)S(1)} %copy-done, bf16[3840,512]{1,0:T(8,128)(2,1)} %param.9), kind=kOutput, calls=%fused_computation.66 | convolution fusion | flops 1006632960 | bytes 6422528 | tf_op jit(solution)/shard_map/dot_general | solution.py:31
  17.0 1.5 copy.38
  18.9 11.4 %reduce-scatter.8.cloned.1.call-done = f32[256,256]{1,0:T(8,128)} async-done(((f32[256,512]{1,0:T(8,128)}), f32[256,256]{1,0:T(8,128)}) %reduce-scatter.8.cloned.1.call-update) | async-done | bytes 262160 | tf_op jit(solution)/shard_map/reduce_scatter | solution.py:33
  31.3 16.1 %all_gather.16 = bf16[1024,256]{1,0:T(8,128)(2,1)} all-gather(bf16[256,256]{1,0:T(8,128)(2,1)S(1)} %convert_element_type.49), channel_id=1, replica_groups=mesh['img'=4,'head'=2,'txt'=4] {'txt'}, dimensions={0}, use_global_device_ids=true | all-gather | bytes 655360 | tf_op jit(solution)/shard_map/all_gather | solution.py:37
  48.6 7.8 %fusion.55 = (f32[2,8,256]{2,1,0:T(8,128)}, f32[2,8,256,1024]{2,3,1,0:T(8,128)}) fusion(bf16[256,2,8,128]{0,3,2,1:T(8,128)(2,1)S(1)} %bitcast.136, bf16[1024,2,128,1]{2,1,0,3:T(2,128)(2,1)S(1)} %bitcast.140, pred[256,1024]{0,1:T(8,128)(4,1)S(1)} %bitcast.139), kind=kOutput, calls=%fused_computation.65 | convolution fusion | flops 1086320640 | bytes 18628608 | tf_op jit(solution)/shard_map/tgrd,jgd->grtj/dot_general | solution.py:51
  56.5 10.7 %pmax.7 = f32[2,8,256]{2,1,0:T(8,128)S(1)} all-reduce(f32[2,8,256]{2,1,0:T(8,128)} %get-tuple-element.8), channel_id=1, replica_groups=mesh['img'=4,'head'=2,'txt'=4] {'img'}, use_global_device_ids=true, to_apply=%region_3.4 | all-reduce | flops 4096 | bytes 32768 | tf_op jit(solution)/shard_map/pmax | solution.py:55
  68.1 17.0 %all_gather.15 = bf16[1024,256]{1,0:T(8,128)(2,1)} all-gather(bf16[256,256]{1,0:T(8,128)(2,1)S(1)} %convert_element_type.47), channel_id=1, replica_groups=mesh['img'=4,'head'=2,'txt'=4] {'txt'}, dimensions={0}, use_global_device_ids=true | all-gather | bytes 655360 | tf_op jit(solution)/shard_map/all_gather | solution.py:38
  86.3 10.0 %fusion.25 = f32[2,128,8,256]{3,1,2,0:T(8,128)} fusion(f32[2,8,256,1024]{2,3,1,0:T(8,128)} %get-tuple-element.9, f32[2,8,256]{2,1,0:T(8,128)S(1)} %pmax.7, bf16[1024,2,128,1]{2,1,0,3:T(2,128)(2,1)S(1)} %bitcast.134), kind=kOutput, calls=%fused_computation.27 | convolution fusion | flops 1082130432 | bytes 19415040 | tf_op jit(solution)/shard_map/grtj,jgd->tgrd/dot_general | solution.py:62
  96.3 3.1 %copy.43 = f32[256,16,128]{2,1,0:T(8,128)} copy(f32[256,16,128]{0,2,1:T(8,128)} %bitcast.135) | data formatting | bytes 4194304 | tf_op jit(solution)/shard_map/reshape | solution.py:65
  99.4 2.3 copy.46
  101.7 9.5 %convert_reduce_fusion = f32[2,8,256]{2,1,0:T(8,128)} fusion(f32[2,8,256,1024]{2,3,1,0:T(8,128)} %get-tuple-element.9, f32[2,8,256]{2,1,0:T(8,128)S(1)} %pmax.7), kind=kLoop, calls=%fused_computation.1 | loop fusion | flops 16773120 | bytes 16809984 | tf_op jit(solution)/shard_map/reduce_sum | solution.py:58
  111.1 12.1 %psum.7 = f32[256,16]{0,1:T(8,128)} all-reduce(f32[256,16]{0,1:T(8,128)} %bitcast.150), channel_id=1, replica_groups=mesh['img'=4,'head'=2,'txt'=4] {'img'}, use_global_device_ids=true, to_apply=%region_6.7 | all-reduce | flops 4096 | bytes 32768 | tf_op jit(solution)/shard_map/psum | solution.py:67
  124.6 1.4 copy.44
  127.4 3.4 %reduce-scatter.10.cloned.1.call-done = f32[64,16,128]{2,1,0:T(8,128)} async-done(((f32[256,16,128]{2,1,0:T(8,128)}), f32[64,16,128]{2,1,0:T(8,128)}) %reduce-scatter.10.cloned.1.call-update) | async-done | bytes 524304 | tf_op jit(solution)/shard_map/reduce_scatter | solution.py:66
  133.9 5.0 %fusion.32 = f32[1024,128]{0,1:T(8,128)S(1)} fusion(f32[2,8,256,1024]{2,3,1,0:T(8,128)} %get-tuple-element.9, f32[8,256]{1,0:T(8,128)S(1)} %get-tuple-element.6, bf16[256,2,8,128]{0,3,2,1:T(8,128)(2,1)} %bitcast.143), kind=kOutput, calls=%fused_computation.31 | convolution fusion | flops 541065216 | bytes 9445376 | tf_op jit(solution)/shard_map/rtj,trd->jd/dot_general | solution.py:95
  138.9 5.2 %fusion.35 = f32[1024,128]{0,1:T(8,128)S(1)} fusion(f32[2,8,256,1024]{2,3,1,0:T(8,128)} %get-tuple-element.9, f32[8,256]{1,0:T(8,128)S(1)} %get-tuple-element.7, bf16[256,2,8,128]{0,3,2,1:T(8,128)(2,1)S(1)} %bitcast.146), kind=kOutput, calls=%fused_computation.32 | convolution fusion | flops 541065216 | bytes 9445376 | tf_op jit(solution)/shard_map/rtj,trd->jd/dot_general | solution.py:95
  145.2 1.7 fusion.53
  147.0 2.7 %all-gather.2.cloned.1.call-done = bf16[256,2048]{1,0:T(8,128)(2,1)} async-done(((bf16[64,2048]{1,0:T(8,128)(2,1)}), bf16[256,2048]{1,0:T(8,128)(2,1)}) %all-gather.2.cloned.1.call-update) | async-done | bytes 1048592 | tf_op jit(solution)/shard_map/all_gather | solution.py:75
  149.7 1.9 multiply_bitcast_fusion
  151.6 1.7 copy.77
  153.4 2.4 %reduce_sum.19 = f32[256,2,8]{2,1,0:T(2,128)S(1)} reduce(f32[256,2,8,128]{3,2,1,0:T(8,128)} %bitcast.133, f32[]{:T(128)} %constant.37.clone.1), dimensions={3}, to_apply=%region_7.8 | reduce | flops 520192 | bytes 2113540 | tf_op jit(solution)/shard_map/reduce_sum | solution.py:78
  156.1 7.9 %fusion.29 = f32[1024,128]{0,1:T(8,128)} fusion(f32[2,8,256,1024]{2,3,1,0:T(8,128)} %get-tuple-element.9, f32[8,256]{1,0:T(8,128)S(1)} %copy.48, f32[8,256]{1,0:T(8,128)} %copy-done.6, bf16[256,2,8,128]{0,3,2,1:T(8,128)(2,1)S(1)} %bitcast.137, bf16[256,2,8,128]{0,3,2,1:T(8,128)(2,1)} %bitcast.144, bf16[1024,1,128]{2,1,0:T(2,128)(2,1)} %get-tuple-element.2), kind=kOutput, calls=%fused_computation.30 | convolution fusion | flops 1084227584 | bytes 10502144 | tf_op jit(solution)/shard_map/rtj,trd->jd/dot_general | solution.py:103
  164.0 7.4 %fusion.26 = f32[1024,128]{0,1:T(8,128)} fusion(f32[2,8,256,1024]{2,3,1,0:T(8,128)} %get-tuple-element.9, f32[8,256]{1,0:T(8,128)S(1)} %copy.52, f32[8,256]{1,0:T(8,128)} %copy-done.5, bf16[256,2,8,128]{0,3,2,1:T(8,128)(2,1)S(1)} %bitcast.138, bf16[256,2,8,128]{0,3,2,1:T(8,128)(2,1)} %bitcast.145, bf16[1024,1,128]{2,1,0:T(2,128)(2,1)S(1)} %copy-done.4), kind=kOutput, calls=%fused_computation.29 | convolution fusion | flops 1084227584 | bytes 10502144 | tf_op jit(solution)/shard_map/rtj,trd->jd/dot_general | solution.py:103
  171.4 2.3 pad_maximum_fusion
  173.7 6.0 %reduce-scatter.14.cloned.1.call-done = f32[256,256]{0,1:T(8,128)} async-done(((f32[1024,256]{0,1:T(8,128)}), f32[256,256]{0,1:T(8,128)}) %reduce-scatter.14.cloned.1.call-update) | async-done | bytes 262160 | tf_op jit(solution)/shard_map/reduce_scatter | solution.py:114
  180.7 5.6 %all_gather.19 = bf16[256,512]{0,1:T(8,128)(2,1)S(1)} all-gather(bf16[256,256]{0,1:T(8,128)(2,1)S(1)} %convert_element_type.60), channel_id=1, replica_groups=mesh['img'=4,'head'=2,'txt'=4] {'head'}, dimensions={1}, use_global_device_ids=true | all-gather | bytes 393216 | tf_op jit(solution)/shard_map/all_gather | solution.py:118
  186.4 22.0 %reduce-scatter.12.cloned.1.call-done = f32[256,256]{0,1:T(8,128)} async-done(((f32[1024,256]{0,1:T(8,128)}), f32[256,256]{0,1:T(8,128)}) %reduce-scatter.12.cloned.1.call-update) | async-done | bytes 262160 | tf_op jit(solution)/shard_map/reduce_scatter | solution.py:113
  209.4 6.0 %all_gather.18 = bf16[256,512]{0,1:T(8,128)(2,1)S(1)} all-gather(bf16[256,256]{0,1:T(8,128)(2,1)S(1)} %convert_element_type.57), channel_id=1, replica_groups=mesh['img'=4,'head'=2,'txt'=4] {'head'}, dimensions={1}, use_global_device_ids=true | all-gather | bytes 393216 | tf_op jit(solution)/shard_map/all_gather | solution.py:117
  215.4 3.4 %fusion.58 = f32[256,3840]{1,0:T(8,128)S(1)} fusion(bf16[256,512]{0,1:T(8,128)(2,1)S(1)} %all_gather.18, bf16[3840,512]{1,0:T(8,128)(2,1)} %param.8), kind=kOutput, calls=%fused_computation.68 | convolution fusion | flops 1006632960 | bytes 8126464 | tf_op jit(solution)/shard_map/dot_general | solution.py:121
  218.9 2.5 %fusion.12 = bf16[256,3840]{1,0:T(8,128)(2,1)} fusion(f32[256,3840]{1,0:T(8,128)S(1)} %fusion.58, bf16[256,512]{0,1:T(8,128)(2,1)S(1)} %all_gather.19, bf16[3840,512]{1,0:T(8,128)(2,1)S(1)} %copy-done.2), kind=kOutput, calls=%fused_computation.20 | convolution fusion | flops 1008599040 | bytes 10092544 | tf_op jit(solution)/shard_map/dot_general | solution.py:122
  (49 shorter events, 15.2 us)
Async XLA Ops:
  7.2 1.6 copy-start
  7.2 11.4 %copy-start.8 = (s32[8]{0:T(128)S(1)}, s32[8]{0:T(128)}, u32[]{:S(2)}) copy-start(s32[8]{0:T(128)} %param.12) | copy-start | bytes 100
  7.2 11.4 %copy-start.7 = (s32[8,8]{1,0:T(8,128)S(1)}, s32[8,8]{1,0:T(8,128)}, u32[]{:S(2)}) copy-start(s32[8,8]{1,0:T(8,128)} %param.13) | copy-start | bytes 772
  7.2 23.1 %reduce-scatter.8.cloned.1.call-start = ((), (), s32[]{:S(2)}) async-start(), calls=%async_computation.6 | async-start | bytes 786432 | tf_op jit(solution)/shard_map/reduce_scatter | solution.py:33
  12.8 54.3 %reduce-scatter.6.cloned.1.call-start = ((), (), s32[]{:S(2)}) async-start(), calls=%async_computation.5 | async-start | bytes 786432 | tf_op jit(solution)/shard_map/reduce_scatter | solution.py:34
  17.0 113.8 %reduce-scatter.10.cloned.1.call-start = ((), (), s32[]{:S(2)}) async-start(), calls=%async_computation.7 | async-start | bytes 2621440 | tf_op jit(solution)/shard_map/reduce_scatter | solution.py:66
  99.4 50.4 %all-gather.2.cloned.1.call-start = ((), (), s32[]{:S(2)}) async-start(), calls=%async_computation.8 | async-start | bytes 1310720 | tf_op jit(solution)/shard_map/all_gather | solution.py:75
  132.9 46.9 %reduce-scatter.14.cloned.1.call-start = ((), (), s32[]{:S(2)}) async-start(), calls=%async_computation.10 | async-start | bytes 1310720 | tf_op jit(solution)/shard_map/reduce_scatter | solution.py:114
  133.1 5.8 %copy-start.3 = (bf16[256,2048]{0,1:T(8,128)(2,1)S(1)}, bf16[256,2048]{0,1:T(8,128)(2,1)}, u32[]{:S(2)}) copy-start(bf16[256,2048]{0,1:T(8,128)(2,1)} %copy.46) | copy-start | bytes 3145732
  133.9 5.0 %copy-start.6 = (f32[8,256]{1,0:T(8,128)}, f32[8,256]{1,0:T(8,128)S(1)}, u32[]{:S(2)}) copy-start(f32[8,256]{1,0:T(8,128)S(1)} %get-tuple-element.6) | copy-start | bytes 24580
  133.9 10.2 %copy-start.5 = (f32[8,256]{1,0:T(8,128)}, f32[8,256]{1,0:T(8,128)S(1)}, u32[]{:S(2)}) copy-start(f32[8,256]{1,0:T(8,128)S(1)} %get-tuple-element.7) | copy-start | bytes 24580
  147.0 61.4 %reduce-scatter.12.cloned.1.call-start = ((), (), s32[]{:S(2)}) async-start(), calls=%async_computation.9 | async-start | bytes 1310720 | tf_op jit(solution)/shard_map/reduce_scatter | solution.py:113
  156.1 7.9 %copy-start.4 = (bf16[1024,1,128]{2,1,0:T(2,128)(2,1)S(1)}, bf16[1024,1,128]{2,1,0:T(2,128)(2,1)}, u32[]{:S(2)}) copy-start(bf16[1024,1,128]{2,1,0:T(2,128)(2,1)} %get-tuple-element.3) | copy-start | bytes 786436
  208.3 10.6 %copy-start.2 = (bf16[3840,512]{1,0:T(8,128)(2,1)S(1)}, bf16[3840,512]{1,0:T(8,128)(2,1)}, u32[]{:S(2)}) copy-start(bf16[3840,512]{1,0:T(8,128)(2,1)} %param.9) | copy-start | bytes 11796484
  215.4 6.0 %copy-start.1 = (bf16[256,2048]{1,0:T(8,128)(2,1)S(1)}, bf16[256,2048]{1,0:T(8,128)(2,1)}, u32[]{:S(2)}) copy-start(bf16[256,2048]{1,0:T(8,128)(2,1)} %all-gather.2.cloned.1.call-done) | copy-start | bytes 3145732
Sparse Core Ops, SparseCore 0:
  12.9 17.3 reduce-scatter.7
  33.1 14.6 reduce-scatter.5
  99.5 31.2 reduce-scatter.9
  133.0 16.7 all-gather.1
  152.4 27.2 reduce-scatter.13
  182.5 25.7 reduce-scatter.11
where the time goes:
time: 230 us; the launch traced here: 229 us
  blocking collectives  67.5 us (29%)
  matrix products  57.8 us (25%)
  waiting for transfers between devices  45.7 us (20%)
  other arithmetic  23.7 us (10%)
  local copies, waits for them, and re-layouts  19.8 us (9%)
  between operations  14.3 us (6%)
    reduce_scatter x1, waiting for transfers between devices, shards(): lax.psum_scatter(key_grad, 'txt', scatter_dimension=0, tiled=True)  22 us
    all_gather x1, blocking collectives, shards(): lax.all_gather(value_own.astype(jnp.bfloat16), 'txt', axis=0, tiled=True)  17 us
    all_gather x1, blocking collectives, shards(): lax.all_gather(key_own.astype(jnp.bfloat16), 'txt', axis=0, tiled=True)  16.1 us
    dot_general x2, matrix products, shards(): jnp.einsum('rtj,trd->jd', grad_scores, query_heads[:, group_index], prefe...  15.3 us
    psum x1, blocking collectives, shards(): totals = lax.psum(local_totals, 'img')  12.1 us
    reduce_scatter x1, waiting for transfers between devices, shards(): lax.psum_scatter(key_part, 'head', scatter_dimension=1, tiled=True)  11.4 us
    pmax x1, blocking collectives, shards(): row_max = lax.pmax(jnp.max(masked, axis=-1), 'img')  10.7 us
    dot_general x2, matrix products, shards(): jnp.einsum('rtj,trd->jd', probabilities.astype(jnp.bfloat16), grad_heads[...  10.2 us
  transfers between devices with their start and end apart: 6, of which 5 were waited for; matrix products, arithmetic and copies ran while one was open for 31% of the time, Pallas kernels for 0%

commit v1 on v0

v1 whole, which is shorter than its diff:
```python
import functools
import math

import jax
import jax.numpy as jnp
from jax import lax
from jax.experimental import pallas as pl
from jax.experimental.pallas import tpu as pltpu
from jax.sharding import PartitionSpec as P

HD = 128
TILE = 128
TBLK = 128
MESH = pl.DeviceIdType.MESH
UNROLL = 4
LOG2E = 1.4426950408889634
NT = (((1,), (1,)), ((), ()))
F32 = jnp.float32
BF16 = jnp.bfloat16


def build_mask(text_sees, tile_image, text_count):
    blocks_total, images_total = text_sees.shape
    text_rows = lax.axis_index("txt") * text_count + jnp.arange(text_count, dtype=jnp.int32)
    block_onehot = (
        (text_rows // TBLK)[:, None] == jnp.arange(blocks_total, dtype=jnp.int32)[None, :]
    ).astype(F32)
    tile_onehot = (
        tile_image[:, None] == jnp.arange(images_total, dtype=jnp.int32)[None, :]
    ).astype(F32)
    tile_sees = jnp.dot(tile_onehot, text_sees.astype(F32).T)
    return jnp.dot(tile_sees, block_onehot.T)


def partner(me, step, count):
    if count & (count - 1):
        return lax.rem(me + step, count)
    other, bit = me, 1
    while bit < count:
        if step & bit:
            other = other + bit - 2 * bit * (lax.rem(other // bit, 2))
        bit *= 2
    return other


def receive_from(me, step, count):
    if count & (count - 1):
        return lax.rem(me - step + count, count)
    return partner(me, step, count)


def kernel(
    sizes,
    feats, kw, vw, q, g, mask,
    attn, dfeats,
    psend, precv, pacc, kvbuf, vtb, sbuf, numt, mst, tst, stbuf, lse, dlt, cown,
    osend, orecv, aout, gsend, grecv, gown, gacc, hall, grelay, facc,
    p_ss, p_rs, kv_ss, kv_rs, st_ss, st_rs, o_ss, o_rs, a_ss, a_rs, g_ss, g_rs, h_ss, h_rs,
    r_ss, gr_ss, gr_rs,
):
    ni, nh, nt = sizes
    img, hd, txt = lax.axis_index("img"), lax.axis_index("head"), lax.axis_index("txt")
    rows = feats.shape[0]
    groups = kvbuf.shape[1] // 2
    own_cols = groups * HD
    heads = q.shape[1] // HD
    reps = heads // groups
    block_tiles = rows // TILE
    share = osend.shape[1]
    relay = nt == 4
    inner = jnp.logical_or(txt == 1, txt == 2)
    outer = jnp.logical_not(inner)
    scale = 1.0 / math.sqrt(HD)
    unroll = math.gcd(UNROLL, reps)

    barrier = pltpu.get_barrier_semaphore()
    for step in range(1, nh):
        pl.semaphore_signal(barrier, inc=1, device_id={"head": lax.rem(hd + step, nh)}, device_id_type=MESH)
    for step in range(1, nt):
        pl.semaphore_signal(barrier, inc=1, device_id={"txt": lax.rem(txt + step, nt)}, device_id_type=MESH)
    for step in range(1, ni):
        pl.semaphore_signal(barrier, inc=1, device_id={"img": lax.rem(img + step, ni)}, device_id_type=MESH)
    pl.semaphore_wait(barrier, nh - 1 + nt - 1 + ni - 1)

    def remote(src, dst, ss, rs, axis, index):
        return pltpu.make_async_remote_copy(
            src_ref=src, dst_ref=dst, send_sem=ss, recv_sem=rs,
            device_id={axis: index}, device_id_type=MESH,
        )

    p_copies = []
    for step in range(1, nh):
        dest = lax.rem(hd + step, nh)
        cols = pl.ds(pl.multiple_of(dest * own_cols, own_cols), own_cols)
        for part, weight in enumerate((kw, vw)):
            psend[step - 1, part] = jnp.dot(
                feats[...], weight[:, cols], preferred_element_type=F32
            ).astype(BF16)
            copy = remote(
                psend.at[step - 1, part], precv.at[step - 1, part],
                p_ss.at[step - 1, part], p_rs.at[step - 1, part], "head", dest,
            )
            copy.start()
            p_copies.append(copy)
    cols = pl.ds(pl.multiple_of(hd * own_cols, own_cols), own_cols)
    for part, weight in enumerate((kw, vw)):
        pacc[part] = jnp.dot(feats[...], weight[:, cols], preferred_element_type=F32)
    kv_copies, relayed = [], []
    for part in range(2):
        total = pacc[part]
        for step in range(1, nh):
            p_copies[(step - 1) * 2 + part].wait_recv()
            total = total + precv[step - 1, part].astype(F32)
        total = total.astype(BF16)
        for group in range(groups):
            kvbuf[txt, part * groups + group] = total[:, group * HD : (group + 1) * HD]
        mine = kvbuf.at[txt, pl.ds(part * groups, groups)]
        for step in range(1, nt):
            copy = remote(
                mine, mine, kv_ss.at[step - 1, part], kv_rs.at[step - 1, part],
                "txt", partner(txt, step, nt),
            )
            if relay and step == 3:
                pl.when(inner)(copy.start)
            else:
                copy.start()
            kv_copies.append(copy)

    for step in range(nt):
        block = receive_from(txt, step, nt)
        if step:
            for part in range(2):
                kv_copies[part * (nt - 1) + step - 1].wait_recv()
                if relay and step == 2:
                    passed = kvbuf.at[block, pl.ds(part * groups, groups)]
                    copy = remote(
                        passed, passed, r_ss.at[part], kv_rs.at[2, part], "txt", partner(txt, 1, nt)
                    )
                    pl.when(inner)(copy.start)
                    relayed.append(copy)
        for group in range(groups):
            vtb[group] = kvbuf[block, groups + group].astype(F32).T.astype(BF16)

        def forward(turn, _, step=step, block=block):
            picked = [turn * unroll + i for i in range(unroll)]
            spans = [pl.ds(pl.multiple_of(head * HD, HD), HD) for head in picked]
            at = [pl.ds(head, 1) for head in picked]
            group = turn * unroll // reps
            keys, values_t = kvbuf[block, group], vtb[group]
            allowed = [
                mask[pl.ds(block * block_tiles + tile, 1), :] > 0.5 for tile in range(block_tiles)
            ]
            if step:
                before = [mst[row, :] for row in at]
                sums = [tst[row, :] for row in at]
                numers = [numt[head] for head in picked]
            kept, tops, totals, outs = [], [], [], []
            for i in range(unroll):
                scores = lax.dot_general(keys, q[:, spans[i]], NT, preferred_element_type=F32)
                scores = scores * (scale * LOG2E)
                masked = jnp.concatenate(
                    [
                        jnp.where(allowed[tile], scores[tile * TILE : (tile + 1) * TILE], -1e30)
                        for tile in range(block_tiles)
                    ],
                    axis=0,
                )
                top = jnp.max(masked, axis=0, keepdims=True)
                if step:
                    top = jnp.maximum(top, before[i])
                kept.append(masked)
                tops.append(top)
            for i in range(unroll):
                weights = jnp.exp2(kept[i] - tops[i]).astype(BF16)
                total = jnp.sum(weights.astype(F32), axis=0, keepdims=True)
                numer = jnp.dot(values_t, weights, preferred_element_type=F32)
                if step:
                    shrink = jnp.exp2(before[i] - tops[i])
                    total = total + sums[i] * shrink
                    numer = numer + numers[i] * shrink
                totals.append(total)
                outs.append(numer)
            for i in range(unroll):
                sbuf[step * heads + picked[i]] = kept[i]
                mst[at[i], :] = tops[i]
                tst[at[i], :] = totals[i]
                numt[picked[i]] = outs[i]
            return 0

        lax.fori_loop(0, heads // unroll, forward, 0)

    def deltas(head, _):
        cols = pl.ds(pl.multiple_of(head * HD, HD), HD)
        grad_t = g[:, cols].astype(F32).T
        row = pl.ds(head, 1)
        stbuf[img, 0, row, :] = mst[row, :]
        stbuf[img, 1, row, :] = tst[row, :]
        stbuf[img, 2, row, :] = jnp.sum(grad_t * numt[head], axis=0, keepdims=True)
        return 0

    lax.fori_loop(0, heads, deltas, 0)
    st_copies = []
    for step in range(1, ni):
        copy = remote(
            stbuf.at[img], stbuf.at[img], st_ss.at[step - 1], st_rs.at[step - 1],
            "img", lax.rem(img + step, ni),
        )
        copy.start()
        st_copies.append(copy)
    for copy in st_copies:
        copy.wait_recv()
    top = stbuf[0, 0]
    for i in range(1, ni):
        top = jnp.maximum(top, stbuf[i, 0])
    total = jnp.zeros_like(top)
    delta = jnp.zeros_like(top)
    for i in range(ni):
        factor = jnp.exp2(stbuf[i, 0] - top)
        total = total + factor * stbuf[i, 1]
        delta = delta + factor * stbuf[i, 2]
    lse[...] = top + jnp.log(total) * LOG2E
    dlt[...] = delta / total
    cown[...] = jnp.exp2(stbuf[img, 0] - top) / total

    def outputs(head, _):
        cols = pl.ds(pl.multiple_of(head * HD, HD), HD)
        piece = (numt[head] * cown[pl.ds(head, 1), :]).T.astype(BF16)
        for i in range(ni):
            osend[i, :, cols] = piece[i * share : (i + 1) * share]
        return 0

    lax.fori_loop(0, heads, outputs, 0)
    o_copies = []
    for step in range(1, ni):
        dest = lax.rem(img + step, ni)
        copy = remote(
            osend.at[dest], orecv.at[step - 1], o_ss.at[step - 1], o_rs.at[step - 1], "img", dest
        )
        copy.start()
        o_copies.append(copy)

    g_copies = []
    for step in range(nt - 1, -1, -1):
        block = receive_from(txt, step, nt)

        for group in range(groups):

            def backward(turn, _, step=step, block=block, group=group):
                picked = [group * reps + turn * unroll + i for i in range(unroll)]
                spans = [pl.ds(pl.multiple_of(head * HD, HD), HD) for head in picked]
                at = [pl.ds(head, 1) for head in picked]
                values = kvbuf[block, groups + group]
                key_grad, value_grad = gacc[0], gacc[1]
                grad_probs = [
                    lax.dot_general(values, g[:, cols], NT, preferred_element_type=F32)
                    for cols in spans
                ]
                for i in range(unroll):
                    probs = jnp.exp2(sbuf[step * heads + picked[i]] - lse[at[i], :])
                    grad_scores = (probs * (grad_probs[i] - dlt[at[i], :])).astype(BF16)
                    key_grad = key_grad + jnp.dot(
                        grad_scores, q[:, spans[i]], preferred_element_type=F32
                    )
                    value_grad = value_grad + jnp.dot(
                        probs.astype(BF16), g[:, spans[i]], preferred_element_type=F32
                    )
                gacc[0] = key_grad
                gacc[1] = value_grad
                return 0

            gacc[...] = jnp.zeros_like(gacc)
            lax.fori_loop(0, reps // unroll, backward, 0)
            if relay and step == 2:
                gown[group] = gacc[0] * scale
                gown[groups + group] = gacc[1]
            elif step:
                gsend[step - 1, group] = (gacc[0] * scale).astype(BF16)
                gsend[step - 1, groups + group] = gacc[1].astype(BF16)
            else:
                gown[group] = gacc[0] * scale
                gown[groups + group] = gacc[1]
        if relay and step == 2:

            def joined():
                relay_up.wait_recv()
                for part in range(2 * groups):
                    gsend[1, part] = (gown[part] + grelay[part].astype(F32)).astype(BF16)

            def alone():
                for part in range(2 * groups):
                    gsend[1, part] = gown[part].astype(BF16)

            pl.when(inner)(joined)
            pl.when(outer)(alone)
        if step:
            copy = remote(
                gsend.at[step - 1], grecv.at[step - 1], g_ss.at[step - 1], g_rs.at[step - 1],
                "txt", block,
            )
            if relay and step == 3:
                relay_up = remote(
                    gsend.at[2], grelay, gr_ss.at[0], gr_rs.at[0], "txt", partner(txt, 1, nt)
                )
                pl.when(inner)(copy.start)
                pl.when(outer)(relay_up.start)
                far = copy
            else:
                copy.start()
                g_copies.append(copy)

    for copy in o_copies:
        copy.wait_recv()
    rows_sum = osend[img].astype(F32)
    for step in range(1, ni):
        rows_sum = rows_sum + orecv[step - 1].astype(F32)
    aout[img] = rows_sum.astype(BF16)
    a_copies = []
    for step in range(1, ni):
        copy = remote(
            aout.at[img], aout.at[img], a_ss.at[step - 1], a_rs.at[step - 1],
            "img", lax.rem(img + step, ni),
        )
        copy.start()
        a_copies.append(copy)

    for copy in g_copies:
        copy.wait_recv()
    for part in range(2 * groups):
        total = gown[part]
        for step in range(1, 3 if relay else nt):
            total = total + grecv[step - 1, part].astype(F32)
        gown[part] = total
    if relay:

        def add_far():
            far.wait_recv()
            for part in range(2 * groups):
                gown[part] = gown[part] + grecv[2, part].astype(F32)

        pl.when(inner)(add_far)
    for part in range(2 * groups):
        hall[hd, part] = gown[part].astype(BF16)
    h_copies = []
    for step in range(1, nh):
        copy = remote(
            hall.at[hd], hall.at[hd], h_ss.at[step - 1], h_rs.at[step - 1],
            "head", lax.rem(hd + step, nh),
        )
        copy.start()
        h_copies.append(copy)
    width = feats.shape[1]
    chunk = math.gcd(width, 768)

    def features(owner):
        cols = pl.ds(pl.multiple_of(owner * own_cols, own_cols), own_cols)
        key_part = jnp.concatenate([hall[owner, i] for i in range(groups)], axis=1)
        value_part = jnp.concatenate([hall[owner, groups + i] for i in range(groups)], axis=1)

        def part(at):
            span = pl.ds(pl.multiple_of(at * chunk, chunk), chunk)
            return span, lax.dot_general(
                key_part, kw[span, cols], NT, preferred_element_type=F32
            ) + lax.dot_general(value_part, vw[span, cols], NT, preferred_element_type=F32)

        return part

    own_part = features(hd)

    def own_features(at, _):
        span, value = own_part(at)
        facc[:, span] = value
        return 0

    lax.fori_loop(0, width // chunk, own_features, 0)
    for step in range(1, nh):
        h_copies[step - 1].wait_recv()
        other_part = features(lax.rem(hd - step + nh, nh))

        def other_features(at, _, step=step, other_part=other_part):
            span, value = other_part(at)
            value = facc[:, span] + value
            if step == nh - 1:
                dfeats[:, span] = value.astype(BF16)
            else:
                facc[:, span] = value
            return 0

        lax.fori_loop(0, width // chunk, other_features, 0)

    for copy in a_copies:
        copy.wait_recv()
    for i in range(ni):
        attn[i] = aout[i]
    near = [copy for at, copy in enumerate(kv_copies) if not (relay and at % (nt - 1) == 2)]
    for copy in p_copies + near + st_copies + o_copies + g_copies + a_copies + h_copies:
        copy.wait_send()
    if relay:

        def inner_sends():
            for copy in [kv_copies[2], kv_copies[5], far] + relayed:
                copy.wait_send()

        pl.when(inner)(inner_sends)
        pl.when(outer)(relay_up.wait_send)


def shards(sizes, image_feats, key_weight, value_weight, queries, grad_out, tile_image, text_sees):
    ni, nh, nt = sizes
    rows = image_feats.shape[0]
    text, width = queries.shape
    heads = width // HD
    own_cols = key_weight.shape[1] // nh
    groups = own_cols // HD
    share = text // ni
    mask = build_mask(text_sees, tile_image, text)
    dma = pltpu.SemaphoreType.DMA
    vmem = pl.BlockSpec(memory_space=pltpu.VMEM)
    attn, grad_feats = pl.pallas_call(
        functools.partial(kernel, sizes),
        out_shape=(
            jax.ShapeDtypeStruct((ni, share, width), BF16),
            jax.ShapeDtypeStruct(image_feats.shape, BF16),
        ),
        in_specs=[vmem] * 6,
        out_specs=(vmem, vmem),
        scratch_shapes=[
            pltpu.VMEM((nh - 1, 2, rows, own_cols), BF16),
            pltpu.VMEM((nh - 1, 2, rows, own_cols), BF16),
            pltpu.VMEM((2, rows, own_cols), F32),
            pltpu.VMEM((nt, 2 * groups, rows, HD), BF16),
            pltpu.VMEM((groups, HD, rows), BF16),
            pltpu.VMEM((nt * heads, rows, text), F32),
            pltpu.VMEM((heads, HD, text), F32),
            pltpu.VMEM((heads, text), F32),
            pltpu.VMEM((heads, text), F32),
            pltpu.VMEM((ni, 3, heads, text), F32),
            pltpu.VMEM((heads, text), F32),
            pltpu.VMEM((heads, text), F32),
            pltpu.VMEM((heads, text), F32),
            pltpu.VMEM((ni, share, width), BF16),
            pltpu.VMEM((ni - 1, share, width), BF16),
            pltpu.VMEM((ni, share, width), BF16),
            pltpu.VMEM((nt - 1, 2 * groups, rows, HD), BF16),
            pltpu.VMEM((nt - 1, 2 * groups, rows, HD), BF16),
            pltpu.VMEM((2 * groups, rows, HD), F32),
            pltpu.VMEM((2, rows, HD), F32),
            pltpu.VMEM((nh, 2 * groups, rows, HD), BF16),
            pltpu.VMEM((2 * groups, rows, HD), BF16),
            pltpu.VMEM((rows, image_feats.shape[1]), F32),
            dma((nh - 1, 2)), dma((nh - 1, 2)),
            dma((nt - 1, 2)), dma((nt - 1, 2)),
            dma((ni - 1,)), dma((ni - 1,)),
            dma((ni - 1,)), dma((ni - 1,)),
            dma((ni - 1,)), dma((ni - 1,)),
            dma((nt - 1,)), dma((nt - 1,)),
            dma((nh - 1,)), dma((nh - 1,)),
            dma((2,)), dma((1,)), dma((1,)),
        ],
        compiler_params=pltpu.CompilerParams(
            collective_id=0, has_side_effects=True, vmem_limit_bytes=60 * 1024 * 1024
        ),
    )(image_feats, key_weight, value_weight, queries, grad_out, mask)
    return (attn.reshape(text, width), grad_feats)


def solution(mesh):
    sizes = (mesh.shape["img"], mesh.shape["head"], mesh.shape["txt"])
    placed = (
        P(("img", "txt"), "head"),
        P("head", None),
        P("head", None),
        P("txt", "head"),
        P("txt", "head"),
        P("img"),
        P(),
    )
    return jax.shard_map(
        functools.partial(shards, sizes),
        mesh=mesh,
        in_specs=placed,
        out_specs=(P("txt", "head"), P(("img", "txt"), "head")),
        check_vma=False,
    )
```

time: 230 us -> 86.5 us (0.38)
  Pallas kernels: 0 us -> 80.3 us
  blocking collectives: 67.5 us -> 0 us
  matrix products: 57.8 us -> 1.6 us
  waiting for transfers between devices: 45.7 us -> 0 us
  other arithmetic: 23.7 us -> 0.01 us
  local copies, waits for them, and re-layouts: 19.8 us -> 3.72 us
  between operations: 14.3 us -> 0.66 us
    pallas_call x0 -> x1, Pallas kernels: none -> 80.3 us  [shards(): pl.pallas_call(functools.partial(kernel, sizes), out_shape=(jax.ShapeDtyp...]
    dot_general x11 -> x1, matrix products: 57.8 us -> 1.6 us  [build_mask(): return jnp.dot(tile_sees, block_onehot.T)]
    all_gather x4 -> x0, blocking collectives: 44.7 us -> none  [the longest x1 17 us: shards(): lax.all_gather(value_own.astype(jnp.bfloat16), 'txt', axis=0, tiled=True)]
    reduce_scatter x5 -> x0, waiting for transfers between devices: 42.9 us -> none  [the longest x1 22 us: shards(): lax.psum_scatter(key_grad, 'txt', scatter_dimension=0, tiled=True)]
    psum x1 -> x0, blocking collectives: 12.1 us -> none  [shards(): totals = lax.psum(local_totals, 'img')]
    reduce_sum x2 -> x0, other arithmetic: 11.8 us -> none  [the longest x1 9.46 us: shards(): jnp.sum(weights, axis=-1, dtype=jnp.float32).transpose(2, 0, 1)]
    pmax x1 -> x0, blocking collectives: 10.7 us -> none  [shards(): row_max = lax.pmax(jnp.max(masked, axis=-1), 'img')]
    reshape x3 -> x0, local copies, waits for them, and re-layouts: 5.42 us -> none  [the longest x1 3.09 us: shards(): numerator = numerator.reshape(text_count, groups * repeats, HD)]
  transfers between devices with their start and end apart: 6 -> 0, of which waited for: 5 -> 0; matrix products, arithmetic and copies ran while one was open for 31% -> 0% of each run, Pallas kernels for 0% -> 0%
where the time goes in v1:
time: 86.5 us; the launch traced here: 86.3 us
  Pallas kernels  80.3 us (93%)
  local copies, waits for them, and re-layouts  3.72 us (4%)
  matrix products  1.6 us (2%)
    pallas_call x1, Pallas kernels, shards(): pl.pallas_call(functools.partial(kernel, sizes), out_shape=(jax.ShapeDtyp...  80.3 us
    unnamed x4, local copies, waits for them, and re-layouts  3.72 us

profile of v1, /device:TPU:0, one launch (start us, length us, event | category | flops | bytes accessed | tf_op | source)
XLA Modules:
  0.0 86.3 jit_solution(3370224738501536936)
XLA Ops:
  0.6 1.6 %fusion.mask = f32[8,256]{1,0:T(8,128)} fusion(s32[256]{0:T(256)S(1)} %and_select_fusion, s32[8,8]{1,0:T(8,128)} %param.13, s32[8]{0:T(128)} %param.12), kind=kOutput, calls=%fused_computation | convolution fusion | flops 35968 | bytes 9504 | tf_op jit(solution)/shard_map/dot_general | solution.py:32
  2.2 80.3 %shard_map.86 = (bf16[4,64,2048]{2,1,0:T(8,128)(2,1)}, bf16[256,3840]{1,0:T(8,128)(2,1)}) custom-call(bf16[256,3840]{1,0:T(8,128)(2,1)} %feats.1, bf16[3840,512]{1,0:T(8,128)(2,1)} %kw.1, bf16[3840,512]{1,0:T(8,128)(2,1)} %vw.1, bf16[256,2048]{1,0:T(8,128)(2,1)} %q.1, bf16[256,2048]{1,0:T(8,128)(2,1)} %g.1, f32[8,256]{1,0:T(8,128)} %fusion.mask), custom_call_target="tpu_custom_call" | custom-call | tf_op jit(solution)/shard_map/pallas_call | solution.py:418
  82.6 0.0 copy-start
  82.6 2.4 %copy.11 = bf16[256,2048]{1,0:T(8,128)(2,1)} copy(bf16[256,2048]{1,0:T(8,128)(2,1)} %bitcast.1) | data formatting | bytes 2097152
  85.0 0.0 copy-done
  85.0 1.3 %copy.12 = bf16[256,3840]{1,0:T(8,128)(2,1)} copy(bf16[256,3840]{1,0:T(8,128)(2,1)S(1)} %copy-done) | data formatting | bytes 3932160
  (1 shorter events, 0.0 us)
Async XLA Ops:
  82.6 2.5 %copy-start = (bf16[256,3840]{1,0:T(8,128)(2,1)S(1)}, bf16[256,3840]{1,0:T(8,128)(2,1)}, u32[]{:S(2)}) copy-start(bf16[256,3840]{1,0:T(8,128)(2,1)} %get-tuple-element.9) | copy-start | bytes 5898244
